TPU v7x, 32 devices: a whole 2x2x4 slice. The times are simulated.
32 devices in a mesh: groups: 2 (over x), ctx: 16 (over z, y, core).
Axes of the slice: x: 2, y: 2, z: 4, core: 2. Of those that a mesh axis runs over, the one named last changes fastest.
Arguments:
- queries: bfloat16 [256, 2048], P(('groups', 'ctx')), parts along dimension 0, may hold values from -200 to 200
- slab_keys: bfloat16 [256, 2048], P(('groups', 'ctx')), parts along dimension 0, may hold values from -6 to 6
- slab_values: bfloat16 [256, 2048], P(('groups', 'ctx')), parts along dimension 0, may hold values from -6 to 6
- cache_keys: bfloat16 [16384, 2048], P(('groups', 'ctx')), parts along dimension 0, may hold values from -12 to 12
- cache_values: bfloat16 [16384, 2048], P(('groups', 'ctx')), parts along dimension 0, may hold values from -6 to 6
- offset: int32 [2], P('groups'), parts along dimension 0, may hold values from 2048 to 8192
- slab_len: int32 [2], P('groups'), parts along dimension 0, may hold values from 64 to 128
Outputs:
- attended: bfloat16 [256, 2048], P(('groups', 'ctx')), parts along dimension 0
There are 2 independent parts, one for each index of `groups`. A program takes and returns all parts, laid end to end along the dimension named above; each array names one. Nothing has to cross between parts.
All inputs are finite; a program needn't handle non-finite values.
Results may differ from a plain program's by a relative error of at most 0.0081.
Values may be sent and summed in bfloat16 or wider, within the bound.
A program may use at most 128 MiB of HBM per device.

v0:
```python
import jax
import jax.numpy as jnp
from jax import lax
from jax.sharding import PartitionSpec as P

DH = 128
KB = 256
very_low = -1e30


def block_state(query_heads, key_blocks, value_blocks, visible, score_scale):
    scores = (
        jnp.einsum("qhd,gkhd->qghk", query_heads, key_blocks, preferred_element_type=jnp.float32)
        * score_scale
    )
    visible_head = visible[:, :, None, :]
    masked = jnp.where(visible_head, scores, very_low)
    maxima = jnp.max(masked, axis=3)
    weights = jnp.exp(jnp.where(visible_head, scores - maxima[..., None], -jnp.inf))
    totals = jnp.sum(weights, axis=3)
    rounded = weights.astype(jnp.bfloat16)
    products = jnp.einsum(
        "qghk,gkhd->qghd", rounded, value_blocks, preferred_element_type=jnp.float32
    )
    return (maxima, totals, products)


def absorb(running, terms):
    largest, weight_sum, weighted = running
    maxima, totals, products = terms
    new_largest = jnp.maximum(largest, jnp.max(maxima, axis=1))
    old_factor = jnp.exp(largest - new_largest)
    factors = jnp.exp(maxima - new_largest[:, None, :])
    weight_sum = weight_sum * old_factor + jnp.sum(factors * totals, axis=1)
    weighted = weighted * old_factor[..., None] + jnp.sum(factors[..., None] * products, axis=1)
    return (new_largest, weight_sum, weighted)


def body(queries, slab_keys, slab_values, cache_keys, cache_values, offset, slab_len):
    device_rank = lax.axis_index("ctx")
    device_count = lax.axis_size("ctx")
    own_rows = queries.shape[0]
    slab_rows = own_rows * device_count
    cache_rows = cache_keys.shape[0]
    head_count = queries.shape[1] // DH
    score_scale = DH ** (-0.5)
    gathered = lax.all_gather(queries, "ctx", axis=0, tiled=True)
    query_heads = gathered.reshape(slab_rows, head_count, DH)
    running = (
        jnp.full((slab_rows, head_count), very_low, jnp.float32),
        jnp.zeros((slab_rows, head_count), jnp.float32),
        jnp.zeros((slab_rows, head_count, DH), jnp.float32),
    )
    for block_number in range(cache_rows // KB):
        block_start = block_number * KB
        key_blocks = cache_keys[block_start : block_start + KB].reshape(1, KB, head_count, DH)
        value_blocks = cache_values[block_start : block_start + KB].reshape(1, KB, head_count, DH)
        positions = device_rank * cache_rows + block_start + jnp.arange(KB, dtype=jnp.int32)
        visible = jnp.broadcast_to((positions < offset[0])[None, None, :], (slab_rows, 1, KB))
        running = absorb(
            running, block_state(query_heads, key_blocks, value_blocks, visible, score_scale)
        )
    own_index = device_rank * own_rows + jnp.arange(own_rows, dtype=jnp.int32)
    largest, weight_sum, weighted = running
    quotient = (weighted / jnp.maximum(weight_sum, 1.0)[..., None]).astype(jnp.bfloat16)
    parts_quotient = lax.all_to_all(
        quotient.reshape(1, slab_rows, head_count * DH),
        "ctx",
        split_axis=1,
        concat_axis=0,
        tiled=True,
    )
    parts_sum, parts_largest = (
        lax.all_to_all(weight_sum[None], "ctx", split_axis=1, concat_axis=0, tiled=True),
        lax.all_to_all(largest[None], "ctx", split_axis=1, concat_axis=0, tiled=True),
    )
    own_largest = jnp.max(parts_largest, axis=0)
    factors = jnp.exp(parts_largest - own_largest[None]) * parts_sum
    own_sum = jnp.sum(factors, axis=0)
    own_weighted = jnp.sum(
        factors[..., None]
        * parts_quotient.reshape(device_count, own_rows, head_count, DH).astype(jnp.float32),
        axis=0,
    )
    own_state = (own_largest, own_sum, own_weighted)
    own_queries = queries.reshape(own_rows, head_count, DH)
    keys_piece = lax.all_gather(slab_keys, "ctx", axis=0, tiled=True)
    values_piece = lax.all_gather(slab_values, "ctx", axis=0, tiled=True)
    piece_rows = keys_piece.shape[0]
    piece_blocks = piece_rows // own_rows
    key_index = jnp.arange(piece_rows, dtype=jnp.int32).reshape(piece_blocks, own_rows)
    visible = (key_index[None] <= own_index[:, None, None]) & (key_index[None] < slab_len[0])
    own_state = absorb(
        own_state,
        block_state(
            own_queries,
            keys_piece.reshape(piece_blocks, own_rows, head_count, DH),
            values_piece.reshape(piece_blocks, own_rows, head_count, DH),
            visible,
            score_scale,
        ),
    )
    final_largest, final_sum, final_weighted = own_state
    combined = (final_weighted / final_sum[..., None]).reshape(own_rows, head_count * DH)
    combined = jnp.where((own_index < slab_len[0])[:, None], combined, 0.0)
    return combined.astype(jnp.bfloat16)


def solution(mesh):
    placed = (
        P(("groups", "ctx"), None),
        P(("groups", "ctx"), None),
        P(("groups", "ctx"), None),
        P(("groups", "ctx"), None),
        P(("groups", "ctx"), None),
        P("groups"),
        P("groups"),
    )
    return jax.shard_map(
        body, mesh=mesh, in_specs=placed, out_specs=P(("groups", "ctx"), None), check_vma=False
    )
```

profile of v0, /device:TPU:0, one launch (start us, length us, event | category | flops | bytes accessed | tf_op | source)
XLA Modules:
  0.0 140.0 jit_solution(13504468689925622335)
XLA Ops:
  0.7 1.7 %fusion.59 = (bf16[256,2048]{1,0:T(8,128)(2,1)S(1)}, bf16[256,2048]{1,0:T(8,128)(2,1)S(1)}) fusion(bf16[512,2048]{1,0:T(8,128)(2,1)} %param.10), kind=kLoop, calls=%fused_computation.94 | loop fusion | bytes 4194304 | tf_op jit(solution)/shard_map/slice | solution.py:56
  2.3 0.5 copy.95
  2.9 0.2 copy-done.5
  3.1 24.6 %all_gather.9 = bf16[128,2048]{1,0:T(8,128)(2,1)S(1)} all-gather(bf16[8,2048]{1,0:T(8,128)(2,1)S(1)} %copy-done.5), channel_id=1, replica_groups=mesh['groups'=2,'ctx'=16] {'ctx'}, dimensions={0}, use_global_device_ids=true | all-gather | bytes 557056 | tf_op jit(solution)/shard_map/all_gather | solution.py:47
  27.7 0.3 copy.62
  28.0 1.3 copy.96
  29.3 0.6 fusion.3
  29.9 0.5 fusion.7
  30.5 0.6 fusion
  31.3 0.5 fusion.9
  31.9 0.5 broadcast.194
  32.3 0.7 reduce.7
  33.0 0.7 reshape.418
  33.7 3.5 %all-to-all-start = ((f32[16,1,128]{2,1,0:T(1,128)}), f32[16,1,128]{2,1,0:T(1,128)S(1)}, u32[]{:S(2)}, u32[]{:S(2)}) async-start(f32[16,1,128]{2,1,0:T(1,128)} %reshape.418), calls=%async_computation | async-start | bytes 16384 | tf_op jit(solution)/shard_map/all_to_all | solution.py:75
  37.9 23.2 %all_gather.10 = bf16[128,2048]{1,0:T(8,128)(2,1)S(1)} all-gather(bf16[8,2048]{1,0:T(8,128)(2,1)S(1)} %copy-done.4), channel_id=1, replica_groups=mesh['groups'=2,'ctx'=16] {'ctx'}, dimensions={0}, use_global_device_ids=true | all-gather | bytes 557056 | tf_op jit(solution)/shard_map/all_gather | solution.py:87
  61.2 0.9 copy.112
  62.1 3.1 %fusion.58 = (bf16[256,2048]{1,0:T(8,128)(2,1)}, bf16[256,2048]{1,0:T(8,128)(2,1)}) fusion(bf16[512,2048]{1,0:T(8,128)(2,1)} %param.11), kind=kLoop, calls=%fused_computation.93 | loop fusion | bytes 4194304 | tf_op jit(solution)/shard_map/slice | solution.py:57
  65.1 1.5 %copy.71 = bf16[256,2048]{0,1:T(8,128)(2,1)S(1)} copy(bf16[256,2048]{1,0:T(8,128)(2,1)} %get-tuple-element.16) | data formatting | bytes 2097152 | tf_op jit(solution)/shard_map/slice | solution.py:57
  66.6 3.3 %fusion.12 = f32[128,1,16,128]{0,3,2,1:T(8,128)} fusion(bf16[256,16,128]{0,2,1:T(8,128)(2,1)S(1)} %bitcast.143, f32[16,256,128]{2,1,0:T(8,128)} %copy-done, f32[128,16]{0,1:T(8,128)S(1)} %get-tuple-element.29, pred[256]{0:T(512)(128)(4,1)S(1)} %get-tuple-element.32, f32[128,16]{0,1:T(8,128)S(1)} %get-tuple-element.23), kind=kOutput, calls=%fused_computation.20 | convolution fusion | flops 136577024 | bytes 4210944 | tf_op jit(solution)/shard_map/qghk,gkhd->qghd/dot_general | solution.py:22
  69.9 3.6 %copy.73 = f32[1,128,2048]{2,0,1:T(1,128)} copy(f32[1,128,2048]{1,2,0:T(8,128)} %bitcast.144) | data formatting | bytes 2097152 | tf_op jit(solution)/shard_map/reduce_sum | solution.py:35
  73.6 1.5 %copy.75 = bf16[256,2048]{0,1:T(8,128)(2,1)S(1)} copy(bf16[256,2048]{1,0:T(8,128)(2,1)} %get-tuple-element.17) | data formatting | bytes 2097152 | tf_op jit(solution)/shard_map/slice | solution.py:57
  75.0 1.8 %fusion.13 = f32[128,1,16,128]{0,3,2,1:T(8,128)} fusion(bf16[256,16,128]{0,2,1:T(8,128)(2,1)S(1)} %bitcast.145, f32[16,256,128]{2,1,0:T(8,128)S(1)} %get-tuple-element.28, f32[128,16]{0,1:T(8,128)S(1)} %get-tuple-element.27, pred[256]{0:T(512)(128)(4,1)S(1)} %get-tuple-element.31, f32[128,16]{0,1:T(8,128)S(1)} %get-tuple-element.15), kind=kOutput, calls=%fused_computation.21 | convolution fusion | flops 136577024 | bytes 4210944 | tf_op jit(solution)/shard_map/qghk,gkhd->qghd/dot_general | solution.py:22
  76.8 2.5 %copy.77 = f32[1,128,2048]{2,0,1:T(1,128)S(1)} copy(f32[1,128,2048]{1,2,0:T(8,128)} %bitcast.146) | data formatting | bytes 2097152 | tf_op jit(solution)/shard_map/reduce_sum | solution.py:35
  79.8 0.5 select_reduce_fusion
  80.3 0.3 mul.193
  80.6 0.3 mul.197
  81.0 0.3 div.29
  81.3 0.2 copy-done.1
  81.5 3.3 %fusion.60 = bf16[128,1,2048]{2,1,0:T(2,128)(2,1)S(1)} fusion(f32[1,128,2048]{2,0,1:T(1,128)S(1)} %bitcast.152, f32[1,128,2048]{2,0,1:T(1,128)S(1)} %copy.77, f32[1,128,2048]{2,0,1:T(1,128)S(1)} %bitcast.151, f32[1,128,2048]{2,0,1:T(1,128)S(1)} %bitcast.150, f32[1,128,2048]{2,0,1:T(1,128)S(1)} %copy-done.1), kind=kLoop, calls=%fused_computation.96 | loop fusion | flops 1310720 | bytes 5767168
  84.8 0.6 fusion.28
  85.5 0.7 reduce.10
  86.2 0.7 reshape.422
  86.9 3.5 %all-to-all-start.1 = ((f32[16,1,128]{2,1,0:T(1,128)}), f32[16,1,128]{2,1,0:T(1,128)S(1)}, u32[]{:S(2)}, u32[]{:S(2)}) async-start(f32[16,1,128]{2,1,0:T(1,128)} %reshape.422), calls=%async_computation.1 | async-start | bytes 16384 | tf_op jit(solution)/shard_map/all_to_all | solution.py:74
  90.4 23.4 %all_gather.11 = bf16[128,2048]{1,0:T(8,128)(2,1)S(1)} all-gather(bf16[8,2048]{1,0:T(8,128)(2,1)S(1)} %copy-done.6), channel_id=1, replica_groups=mesh['groups'=2,'ctx'=16] {'ctx'}, dimensions={0}, use_global_device_ids=true | all-gather | bytes 557056 | tf_op jit(solution)/shard_map/all_gather | solution.py:88
  113.9 0.5 broadcast.196
  114.4 3.7 %reduce.9 = bf16[128,2048]{1,0:T(8,128)(2,1)S(1)} reduce(bf16[128,1,2048]{2,1,0:T(2,128)(2,1)S(1)} %fusion.60, bf16[]{:T(256)} %broadcast.196), dimensions={1}, to_apply=%fusion.60.reduce_sub_computation | reduce | bytes 1048578
  118.1 1.3 reshape.420
  119.4 3.6 %all-to-all-start.2 = ((bf16[16,2,8192]{2,1,0:T(2,128)(2,1)}), bf16[16,2,8192]{2,1,0:T(2,128)(2,1)S(1)}, u32[]{:S(2)}, u32[]{:S(2)}) async-start(bf16[16,2,8192]{2,1,0:T(2,128)(2,1)} %reshape.420), calls=%async_computation.2 | async-start | bytes 1048576 | tf_op jit(solution)/shard_map/all_to_all | solution.py:66
  123.0 0.6 reduce.8
  123.6 0.1 reshape.419
  123.8 0.6 reduce.11
  124.3 0.1 reshape.423
  124.8 0.6 fusion.14
  125.4 11.8 %all-to-all-done.2 = bf16[16,2,8192]{2,1,0:T(2,128)(2,1)S(1)} async-done(((bf16[16,2,8192]{2,1,0:T(2,128)(2,1)}), bf16[16,2,8192]{2,1,0:T(2,128)(2,1)S(1)}, u32[]{:S(2)}, u32[]{:S(2)}) %all-to-all-start.2) | async-done | bytes 524320 | tf_op jit(solution)/shard_map/all_to_all | solution.py:66
  137.3 0.5 reshape.421
  137.8 1.1 bitcast_convert_fusion
  138.9 0.4 multiply_reduce_fusion
  139.3 0.7 fusion.33
  (37 shorter events, 1.4 us)
Async XLA Ops:
  2.3 0.8 copy-start.5
  29.3 1.2 copy-start.2
  29.9 1.4 copy-start
  31.3 6.7 %copy-start.4 = (bf16[8,2048]{1,0:T(8,128)(2,1)S(1)}, bf16[8,2048]{1,0:T(8,128)(2,1)}, u32[]{:S(2)}) copy-start(bf16[8,2048]{1,0:T(8,128)(2,1)} %param.8) | copy-start | bytes 98308
  33.7 53.2 %all-to-all-start = ((f32[16,1,128]{2,1,0:T(1,128)}), f32[16,1,128]{2,1,0:T(1,128)S(1)}, u32[]{:S(2)}, u32[]{:S(2)}) async-start(f32[16,1,128]{2,1,0:T(1,128)} %reshape.418), calls=%async_computation | async-start | bytes 16384 | tf_op jit(solution)/shard_map/all_to_all | solution.py:75
  76.8 2.9 %copy-start.3 = (bf16[16,8,16,128]{3,2,1,0:T(8,128)(2,1)S(1)}, bf16[16,8,16,128]{3,2,1,0:T(8,128)(2,1)}, u32[]{:S(2)}) copy-start(bf16[16,8,16,128]{3,2,1,0:T(8,128)(2,1)} %copy.112) | copy-start | bytes 1572868
  80.3 1.2 copy-start.1
  84.8 5.6 %copy-start.6 = (bf16[8,2048]{1,0:T(8,128)(2,1)S(1)}, bf16[8,2048]{1,0:T(8,128)(2,1)}, u32[]{:S(2)}) copy-start(bf16[8,2048]{1,0:T(8,128)(2,1)} %param.9) | copy-start | bytes 98308
  86.9 32.5 %all-to-all-start.1 = ((f32[16,1,128]{2,1,0:T(1,128)}), f32[16,1,128]{2,1,0:T(1,128)S(1)}, u32[]{:S(2)}, u32[]{:S(2)}) async-start(f32[16,1,128]{2,1,0:T(1,128)} %reshape.422), calls=%async_computation.1 | async-start | bytes 16384 | tf_op jit(solution)/shard_map/all_to_all | solution.py:74
  119.4 17.8 %all-to-all-start.2 = ((bf16[16,2,8192]{2,1,0:T(2,128)(2,1)}), bf16[16,2,8192]{2,1,0:T(2,128)(2,1)S(1)}, u32[]{:S(2)}, u32[]{:S(2)}) async-start(bf16[16,2,8192]{2,1,0:T(2,128)(2,1)} %reshape.420), calls=%async_computation.2 | async-start | bytes 1048576 | tf_op jit(solution)/shard_map/all_to_all | solution.py:66
where the time goes:
time: 141 us; the launch traced here: 140 us
  blocking collectives  71.2 us (50%)
  local copies, waits for them, and re-layouts  23.8 us (17%)
  other arithmetic  13.6 us (10%)
  waiting for transfers between devices  11.9 us (8%)
  starting transfers between devices  10.5 us (7%)
  matrix products  7.41 us (5%)
  between operations  1.62 us (1%)
    all_gather x1, blocking collectives, body(): gathered = lax.all_gather(queries, 'ctx', axis=0, tiled=True)  24.6 us
    all_gather x1, blocking collectives, body(): values_piece = lax.all_gather(slab_values, 'ctx', axis=0, tiled=True)  23.4 us
    all_gather x1, blocking collectives, body(): keys_piece = lax.all_gather(slab_keys, 'ctx', axis=0, tiled=True)  23.2 us
    all_to_all x1, waiting for transfers between devices, body(): lax.all_to_all(quotient.reshape(1, slab_rows, head_count * DH), 'ctx', sp...  11.8 us
    unnamed x5, other arithmetic  8.48 us
    unnamed x25, local copies, waits for them, and re-layouts  7.98 us
    reduce_sum x2, local copies, waits for them, and re-layouts, absorb(): jnp.sum(factors[..., None] * products, axis=1)  6.12 us
    slice x3, local copies, waits for them, and re-layouts, body(): cache_values[block_start:block_start + KB].reshape(1, KB, head_count, DH)  6.04 us
  transfers between devices with their start and end apart: 3, of which 1 were waited for; matrix products, arithmetic and copies ran while one was open for 24% of the time, Pallas kernels for 0%

commit v1 on v0

--- a/solution.py
+++ b/solution.py
@@ -6,6 +6,19 @@
 DH = 128
 KB = 256
 very_low = -1e30
+
+
+def collect(x, axis, dim):
+    length, position, rows = (lax.axis_size(axis), lax.axis_index(axis), x.shape[dim])
+    upward = [(i, (i + 1) % length) for i in range(length)]
+    filled = jnp.zeros((*x.shape[:dim], length * rows, *x.shape[dim + 1 :]), x.dtype)
+    current = x
+    for step in range(length):
+        owner = (position - step) % length
+        filled = lax.dynamic_update_slice_in_dim(filled, current, owner * rows, axis=dim)
+        if step < length - 1:
+            current = lax.ppermute(current, axis, upward)
+    return filled
 
 
 def block_state(query_heads, key_blocks, value_blocks, visible, score_scale):
@@ -85,7 +98,7 @@
     own_state = (own_largest, own_sum, own_weighted)
     own_queries = queries.reshape(own_rows, head_count, DH)
     keys_piece = lax.all_gather(slab_keys, "ctx", axis=0, tiled=True)
-    values_piece = lax.all_gather(slab_values, "ctx", axis=0, tiled=True)
+    values_piece = collect(slab_values, "ctx", 0)
     piece_rows = keys_piece.shape[0]
     piece_blocks = piece_rows // own_rows
     key_index = jnp.arange(piece_rows, dtype=jnp.int32).reshape(piece_blocks, own_rows)

time: 141 us -> 204 us (1.45)
  waiting for transfers between devices: 11.9 us -> 90.4 us
  blocking collectives: 71.2 us -> 47.6 us
  starting transfers between devices: 10.5 us -> 13.7 us
  local copies, waits for them, and re-layouts: 23.8 us -> 26.9 us
    ppermute x0 -> x15, waiting for transfers between devices: none -> 90.4 us  [collect(): current = lax.ppermute(current, axis, upward)]
    all_gather x1 -> x0, blocking collectives: 23.4 us -> none  [body(): values_piece = lax.all_gather(slab_values, 'ctx', axis=0, tiled=True)]
    all_to_all x1, waiting for transfers between devices: 11.8 us -> 0.01 us  [body(): lax.all_to_all(quotient.reshape(1, slab_rows, head_count * DH), 'ctx', sp...]
    all_to_all x1, starting transfers between devices: 3.57 us -> 5.8 us  [body(): lax.all_to_all(quotient.reshape(1, slab_rows, head_count * DH), 'ctx', sp...]
    unnamed x25 -> x27, local copies, waits for them, and re-layouts: 7.98 us -> 7.88 us
  transfers between devices with their start and end apart: 3 -> 18, of which waited for: 1 -> 14; matrix products, arithmetic and copies ran while one was open for 24% -> 19% of each run, Pallas kernels for 0% -> 0%
where the time goes in v1:
time: 204 us; the launch traced here: 203 us
  waiting for transfers between devices  90.4 us (44%)
  blocking collectives  47.6 us (23%)
  local copies, waits for them, and re-layouts  26.9 us (13%)
  other arithmetic  15.4 us (8%)
  starting transfers between devices  13.7 us (7%)
  matrix products  7.41 us (4%)
    ppermute x15, waiting for transfers between devices, collect(): current = lax.ppermute(current, axis, upward)  90.4 us
    all_gather x1, blocking collectives, body(): gathered = lax.all_gather(queries, 'ctx', axis=0, tiled=True)  24.6 us
    all_gather x1, blocking collectives, body(): keys_piece = lax.all_gather(slab_keys, 'ctx', axis=0, tiled=True)  23 us
    unnamed x5, other arithmetic  9.1 us
    unnamed x27, local copies, waits for them, and re-layouts  7.88 us
    reduce_sum x2, local copies, waits for them, and re-layouts, absorb(): jnp.sum(factors[..., None] * products, axis=1)  6.12 us
    slice x3, local copies, waits for them, and re-layouts, body(): cache_values[block_start:block_start + KB].reshape(1, KB, head_count, DH)  6.04 us
    all_to_all x1, starting transfers between devices, body(): lax.all_to_all(quotient.reshape(1, slab_rows, head_count * DH), 'ctx', sp...  5.8 us
  transfers between devices with their start and end apart: 18, of which 14 were waited for; matrix products, arithmetic and copies ran while one was open for 19% of the time, Pallas kernels for 0%

profile of v1, /device:TPU:0, one launch (start us, length us, event | category | flops | bytes accessed | tf_op | source)
XLA Modules:
  0.0 203.4 jit_solution(10085835974880276209)
XLA Ops:
  0.7 1.7 fusion.59
  3.1 24.6 %all_gather.6 = bf16[128,2048]{1,0:T(8,128)(2,1)S(1)} all-gather(bf16[8,2048]{1,0:T(8,128)(2,1)S(1)} %copy-done.6), channel_id=1, replica_groups=mesh['groups'=2,'ctx'=16] {'ctx'}, dimensions={0}, use_global_device_ids=true | all-gather | bytes 557056 | tf_op jit(solution)/shard_map/all_gather | solution.py:60
  28.0 1.3 copy.96
  29.4 0.6 fusion.3
  30.6 0.6 fusion
  31.8 0.6 fusion.41
  33.0 0.7 reduce.7
  33.7 0.7 reshape.418
  34.4 3.5 %all-to-all-start = ((f32[16,1,128]{2,1,0:T(1,128)}), f32[16,1,128]{2,1,0:T(1,128)S(1)}, u32[]{:S(2)}, u32[]{:S(2)}) async-start(f32[16,1,128]{2,1,0:T(1,128)} %reshape.418), calls=%async_computation | async-start | bytes 16384 | tf_op jit(solution)/shard_map/all_to_all | solution.py:88
  38.9 23.0 %all_gather.7 = bf16[128,2048]{1,0:T(8,128)(2,1)S(1)} all-gather(bf16[8,2048]{1,0:T(8,128)(2,1)S(1)} %copy-done.5), channel_id=1, replica_groups=mesh['groups'=2,'ctx'=16] {'ctx'}, dimensions={0}, use_global_device_ids=true | all-gather | bytes 557056 | tf_op jit(solution)/shard_map/all_gather | solution.py:100
  62.0 0.9 copy.112
  62.9 3.1 %fusion.58 = (bf16[256,2048]{1,0:T(8,128)(2,1)}, bf16[256,2048]{1,0:T(8,128)(2,1)}) fusion(bf16[512,2048]{1,0:T(8,128)(2,1)} %param.11), kind=kLoop, calls=%fused_computation.109 | loop fusion | bytes 4194304 | tf_op jit(solution)/shard_map/slice | solution.py:70
  65.9 1.5 copy.71
  67.4 3.3 %fusion.12 = f32[128,1,16,128]{0,3,2,1:T(8,128)} fusion(bf16[256,16,128]{0,2,1:T(8,128)(2,1)S(1)} %bitcast.143, f32[16,256,128]{2,1,0:T(8,128)} %copy-done, f32[128,16]{0,1:T(8,128)S(1)} %get-tuple-element.29, pred[256]{0:T(512)(128)(4,1)S(1)} %get-tuple-element.32, f32[128,16]{0,1:T(8,128)S(1)} %get-tuple-element.23), kind=kOutput, calls=%fused_computation.20 | convolution fusion | flops 136577024 | bytes 4210944 | tf_op jit(solution)/shard_map/qghk,gkhd->qghd/dot_general | solution.py:35
  70.7 3.6 %copy.73 = f32[1,128,2048]{2,0,1:T(1,128)} copy(f32[1,128,2048]{1,2,0:T(8,128)} %bitcast.144) | data formatting | bytes 2097152 | tf_op jit(solution)/shard_map/reduce_sum | solution.py:48
  74.4 1.5 copy.75
  75.8 1.8 fusion.13
  77.6 2.5 %copy.77 = f32[1,128,2048]{2,0,1:T(1,128)S(1)} copy(f32[1,128,2048]{1,2,0:T(8,128)} %bitcast.146) | data formatting | bytes 2097152 | tf_op jit(solution)/shard_map/reduce_sum | solution.py:48
  80.3 0.7 copy.78
  81.7 1.2 fusion.28
  83.5 1.2 div.29
  84.7 3.8 %fusion.60 = bf16[128,1,2048]{2,1,0:T(2,128)(2,1)S(1)} fusion(f32[1,128,2048]{2,0,1:T(1,128)S(1)} %bitcast.152, f32[1,128,2048]{2,0,1:T(1,128)S(1)} %copy.77, f32[1,128,2048]{2,0,1:T(1,128)S(1)} %bitcast.151, f32[1,128,2048]{2,0,1:T(1,128)S(1)} %bitcast.150, f32[1,128,2048]{2,0,1:T(1,128)S(1)} %copy-done.1), kind=kLoop, calls=%fused_computation.112 | loop fusion | flops 1310720 | bytes 5767168
  88.6 0.8 constant_dynamic-update-slice_fusion.15
  89.5 0.7 reduce.10
  90.2 0.7 reshape.422
  90.9 3.7 %all-to-all-start.1 = ((f32[16,1,128]{2,1,0:T(1,128)}), f32[16,1,128]{2,1,0:T(1,128)S(1)}, u32[]{:S(2)}, u32[]{:S(2)}) async-start(f32[16,1,128]{2,1,0:T(1,128)} %reshape.422), calls=%async_computation.1 | async-start | bytes 16384 | tf_op jit(solution)/shard_map/all_to_all | solution.py:87
  95.5 3.7 %reduce.9 = bf16[128,2048]{1,0:T(8,128)(2,1)S(1)} reduce(bf16[128,1,2048]{2,1,0:T(2,128)(2,1)S(1)} %fusion.60, bf16[]{:T(256)} %broadcast.212), dimensions={1}, to_apply=%fusion.60.reduce_sub_computation | reduce | bytes 1048578
  99.3 1.3 reshape.420
  100.6 0.6 reduce.8
  101.4 5.8 %all-to-all-start.2 = ((bf16[16,2,8192]{2,1,0:T(2,128)(2,1)}), bf16[16,2,8192]{2,1,0:T(2,128)(2,1)S(1)}, u32[]{:S(2)}, u32[]{:S(2)}) async-start(bf16[16,2,8192]{2,1,0:T(2,128)(2,1)} %reshape.420), calls=%async_computation.2 | async-start | bytes 1048576 | tf_op jit(solution)/shard_map/all_to_all | solution.py:79
  107.2 0.6 reduce.11
  108.7 0.8 constant_dynamic-update-slice_fusion.14
  109.5 12.1 %collective-permute-done.1 = bf16[8,2048]{1,0:T(8,128)(2,1)S(1)} collective-permute-done((bf16[8,2048]{1,0:T(8,128)(2,1)}, bf16[8,2048]{1,0:T(8,128)(2,1)S(1)}, u32[]{:S(2)}, u32[]{:S(2)}) %collective-permute-start.1) | collective-permute-done | bytes 32800 | tf_op jit(solution)/shard_map/ppermute | solution.py:20
  121.6 6.0 %collective-permute-done.2 = bf16[8,2048]{1,0:T(8,128)(2,1)S(1)} collective-permute-done((bf16[8,2048]{1,0:T(8,128)(2,1)S(1)}, bf16[8,2048]{1,0:T(8,128)(2,1)S(1)}, u32[]{:S(2)}, u32[]{:S(2)}) %collective-permute-start.2) | collective-permute-done | bytes 32800 | tf_op jit(solution)/shard_map/ppermute | solution.py:20
  127.6 6.0 %collective-permute-done.3 = bf16[8,2048]{1,0:T(8,128)(2,1)S(1)} collective-permute-done((bf16[8,2048]{1,0:T(8,128)(2,1)S(1)}, bf16[8,2048]{1,0:T(8,128)(2,1)S(1)}, u32[]{:S(2)}, u32[]{:S(2)}) %collective-permute-start.3) | collective-permute-done | bytes 32800 | tf_op jit(solution)/shard_map/ppermute | solution.py:20
  133.6 6.0 %collective-permute-done.4 = bf16[8,2048]{1,0:T(8,128)(2,1)S(1)} collective-permute-done((bf16[8,2048]{1,0:T(8,128)(2,1)S(1)}, bf16[8,2048]{1,0:T(8,128)(2,1)S(1)}, u32[]{:S(2)}, u32[]{:S(2)}) %collective-permute-start.4) | collective-permute-done | bytes 32800 | tf_op jit(solution)/shard_map/ppermute | solution.py:20
  139.7 6.0 %collective-permute-done.5 = bf16[8,2048]{1,0:T(8,128)(2,1)S(1)} collective-permute-done((bf16[8,2048]{1,0:T(8,128)(2,1)S(1)}, bf16[8,2048]{1,0:T(8,128)(2,1)S(1)}, u32[]{:S(2)}, u32[]{:S(2)}) %collective-permute-start.5) | collective-permute-done | bytes 32800 | tf_op jit(solution)/shard_map/ppermute | solution.py:20
  145.7 6.0 %collective-permute-done.6 = bf16[8,2048]{1,0:T(8,128)(2,1)S(1)} collective-permute-done((bf16[8,2048]{1,0:T(8,128)(2,1)S(1)}, bf16[8,2048]{1,0:T(8,128)(2,1)S(1)}, u32[]{:S(2)}, u32[]{:S(2)}) %collective-permute-start.6) | collective-permute-done | bytes 32800 | tf_op jit(solution)/shard_map/ppermute | solution.py:20
  151.8 6.0 %collective-permute-done.7 = bf16[8,2048]{1,0:T(8,128)(2,1)S(1)} collective-permute-done((bf16[8,2048]{1,0:T(8,128)(2,1)S(1)}, bf16[8,2048]{1,0:T(8,128)(2,1)S(1)}, u32[]{:S(2)}, u32[]{:S(2)}) %collective-permute-start.7) | collective-permute-done | bytes 32800 | tf_op jit(solution)/shard_map/ppermute | solution.py:20
  157.8 6.0 %collective-permute-done.8 = bf16[8,2048]{1,0:T(8,128)(2,1)S(1)} collective-permute-done((bf16[8,2048]{1,0:T(8,128)(2,1)S(1)}, bf16[8,2048]{1,0:T(8,128)(2,1)S(1)}, u32[]{:S(2)}, u32[]{:S(2)}) %collective-permute-start.8) | collective-permute-done | bytes 32800 | tf_op jit(solution)/shard_map/ppermute | solution.py:20
  163.8 6.0 %collective-permute-done.9 = bf16[8,2048]{1,0:T(8,128)(2,1)S(1)} collective-permute-done((bf16[8,2048]{1,0:T(8,128)(2,1)S(1)}, bf16[8,2048]{1,0:T(8,128)(2,1)S(1)}, u32[]{:S(2)}, u32[]{:S(2)}) %collective-permute-start.9) | collective-permute-done | bytes 32800 | tf_op jit(solution)/shard_map/ppermute | solution.py:20
  169.9 6.0 %collective-permute-done.10 = bf16[8,2048]{1,0:T(8,128)(2,1)S(1)} collective-permute-done((bf16[8,2048]{1,0:T(8,128)(2,1)S(1)}, bf16[8,2048]{1,0:T(8,128)(2,1)S(1)}, u32[]{:S(2)}, u32[]{:S(2)}) %collective-permute-start.10) | collective-permute-done | bytes 32800 | tf_op jit(solution)/shard_map/ppermute | solution.py:20
  175.9 6.0 %collective-permute-done.11 = bf16[8,2048]{1,0:T(8,128)(2,1)S(1)} collective-permute-done((bf16[8,2048]{1,0:T(8,128)(2,1)S(1)}, bf16[8,2048]{1,0:T(8,128)(2,1)S(1)}, u32[]{:S(2)}, u32[]{:S(2)}) %collective-permute-start.11) | collective-permute-done | bytes 32800 | tf_op jit(solution)/shard_map/ppermute | solution.py:20
  181.9 6.0 %collective-permute-done.12 = bf16[8,2048]{1,0:T(8,128)(2,1)S(1)} collective-permute-done((bf16[8,2048]{1,0:T(8,128)(2,1)S(1)}, bf16[8,2048]{1,0:T(8,128)(2,1)S(1)}, u32[]{:S(2)}, u32[]{:S(2)}) %collective-permute-start.12) | collective-permute-done | bytes 32800 | tf_op jit(solution)/shard_map/ppermute | solution.py:20
  188.0 6.0 %collective-permute-done.13 = bf16[8,2048]{1,0:T(8,128)(2,1)S(1)} collective-permute-done((bf16[8,2048]{1,0:T(8,128)(2,1)S(1)}, bf16[8,2048]{1,0:T(8,128)(2,1)S(1)}, u32[]{:S(2)}, u32[]{:S(2)}) %collective-permute-start.13) | collective-permute-done | bytes 32800 | tf_op jit(solution)/shard_map/ppermute | solution.py:20
  194.0 6.0 %collective-permute-done.14 = bf16[8,2048]{1,0:T(8,128)(2,1)S(1)} collective-permute-done((bf16[8,2048]{1,0:T(8,128)(2,1)S(1)}, bf16[8,2048]{1,0:T(8,128)(2,1)S(1)}, u32[]{:S(2)}, u32[]{:S(2)}) %collective-permute-start.14) | collective-permute-done | bytes 32800 | tf_op jit(solution)/shard_map/ppermute | solution.py:20
  201.2 1.1 bitcast_convert_fusion
  202.7 0.7 fusion.33
  (85 shorter events, 8.2 us)
Async XLA Ops:
  2.4 0.8 copy-start.6
  29.3 1.2 copy-start.2
  30.0 1.4 copy-start
  31.3 7.6 %copy-start.5 = (bf16[8,2048]{1,0:T(8,128)(2,1)S(1)}, bf16[8,2048]{1,0:T(8,128)(2,1)}, u32[]{:S(2)}) copy-start(bf16[8,2048]{1,0:T(8,128)(2,1)} %param.8) | copy-start | bytes 98308
  34.4 56.5 %all-to-all-start = ((f32[16,1,128]{2,1,0:T(1,128)}), f32[16,1,128]{2,1,0:T(1,128)S(1)}, u32[]{:S(2)}, u32[]{:S(2)}) async-start(f32[16,1,128]{2,1,0:T(1,128)} %reshape.418), calls=%async_computation | async-start | bytes 16384 | tf_op jit(solution)/shard_map/all_to_all | solution.py:88
  37.9 70.3 %collective-permute-start = (bf16[8,2048]{1,0:T(8,128)(2,1)}, bf16[8,2048]{1,0:T(8,128)(2,1)}, u32[]{:S(2)}, u32[]{:S(2)}) collective-permute-start(bf16[8,2048]{1,0:T(8,128)(2,1)} %param.9), channel_id=1, source_target_pairs={{0,1},{1,2},{2,3},{3,4},{4,5},{5,6},{6,7},{7,8},{8,9},{9,10},{10,1... | collective-permute-start | bytes 98312 | tf_op jit(solution)/shard_map/ppermute | solution.py:20
  77.6 3.5 %copy-start.4 = (bf16[16,8,16,128]{3,2,1,0:T(8,128)(2,1)S(1)}, bf16[16,8,16,128]{3,2,1,0:T(8,128)(2,1)}, u32[]{:S(2)}) copy-start(bf16[16,8,16,128]{3,2,1,0:T(8,128)(2,1)} %copy.112) | copy-start | bytes 1572868
  82.9 1.8 copy-start.1
  84.7 4.7 %copy-start.7 = (f32[1,128,16]{1,2,0:T(8,128)S(1)}, f32[1,128,16]{1,2,0:T(8,128)}, u32[]{:S(2)}) copy-start(f32[1,128,16]{1,2,0:T(8,128)} %get-tuple-element.21) | copy-start | bytes 24580
  90.9 10.4 %all-to-all-start.1 = ((f32[16,1,128]{2,1,0:T(1,128)}), f32[16,1,128]{2,1,0:T(1,128)S(1)}, u32[]{:S(2)}, u32[]{:S(2)}) async-start(f32[16,1,128]{2,1,0:T(1,128)} %reshape.422), calls=%async_computation.1 | async-start | bytes 16384 | tf_op jit(solution)/shard_map/all_to_all | solution.py:87
  99.3 100.8 %copy-start.3 = (bf16[8,16,16,8]{0,3,1,2:T(8,128)(2,1)S(1)}, bf16[8,16,16,8]{0,3,1,2:T(8,128)(2,1)}, u32[]{:S(2)}) copy-start(bf16[8,16,16,8]{0,3,1,2:T(8,128)(2,1)} %get-tuple-element.20) | copy-start | bytes 98308
  101.4 99.3 %all-to-all-start.2 = ((bf16[16,2,8192]{2,1,0:T(2,128)(2,1)}), bf16[16,2,8192]{2,1,0:T(2,128)(2,1)S(1)}, u32[]{:S(2)}, u32[]{:S(2)}) async-start(bf16[16,2,8192]{2,1,0:T(2,128)(2,1)} %reshape.420), calls=%async_computation.2 | async-start | bytes 1048576 | tf_op jit(solution)/shard_map/all_to_all | solution.py:79
  108.2 13.3 %collective-permute-start.1 = (bf16[8,2048]{1,0:T(8,128)(2,1)}, bf16[8,2048]{1,0:T(8,128)(2,1)S(1)}, u32[]{:S(2)}, u32[]{:S(2)}) collective-permute-start(bf16[8,2048]{1,0:T(8,128)(2,1)} %collective-permute-done), channel_id=1, source_target_pairs={{0,1},{1,2},{2,3},{3,4},{4,5},{5,6},{6,7},{7,8},{8,9},{9,10},{10,1... | collective-permute-start | bytes 98312 | tf_op jit(solution)/shard_map/ppermute | solution.py:20
  121.6 6.0 %collective-permute-start.2 = (bf16[8,2048]{1,0:T(8,128)(2,1)S(1)}, bf16[8,2048]{1,0:T(8,128)(2,1)S(1)}, u32[]{:S(2)}, u32[]{:S(2)}) collective-permute-start(bf16[8,2048]{1,0:T(8,128)(2,1)S(1)} %collective-permute-done.1), channel_id=1, source_target_pairs={{0,1},{1,2},{2,3},{3,4},{4,5},{5,6},{6,7},{7,8},{8,9},{9,10},{10,1... | collective-permute-start | bytes 98312 | tf_op jit(solution)/shard_map/ppermute | solution.py:20
  127.6 6.0 %collective-permute-start.3 = (bf16[8,2048]{1,0:T(8,128)(2,1)S(1)}, bf16[8,2048]{1,0:T(8,128)(2,1)S(1)}, u32[]{:S(2)}, u32[]{:S(2)}) collective-permute-start(bf16[8,2048]{1,0:T(8,128)(2,1)S(1)} %collective-permute-done.2), channel_id=1, source_target_pairs={{0,1},{1,2},{2,3},{3,4},{4,5},{5,6},{6,7},{7,8},{8,9},{9,10},{10,1... | collective-permute-start | bytes 98312 | tf_op jit(solution)/shard_map/ppermute | solution.py:20
  133.6 6.0 %collective-permute-start.4 = (bf16[8,2048]{1,0:T(8,128)(2,1)S(1)}, bf16[8,2048]{1,0:T(8,128)(2,1)S(1)}, u32[]{:S(2)}, u32[]{:S(2)}) collective-permute-start(bf16[8,2048]{1,0:T(8,128)(2,1)S(1)} %collective-permute-done.3), channel_id=1, source_target_pairs={{0,1},{1,2},{2,3},{3,4},{4,5},{5,6},{6,7},{7,8},{8,9},{9,10},{10,1... | collective-permute-start | bytes 98312 | tf_op jit(solution)/shard_map/ppermute | solution.py:20
  139.7 6.0 %collective-permute-start.5 = (bf16[8,2048]{1,0:T(8,128)(2,1)S(1)}, bf16[8,2048]{1,0:T(8,128)(2,1)S(1)}, u32[]{:S(2)}, u32[]{:S(2)}) collective-permute-start(bf16[8,2048]{1,0:T(8,128)(2,1)S(1)} %collective-permute-done.4), channel_id=1, source_target_pairs={{0,1},{1,2},{2,3},{3,4},{4,5},{5,6},{6,7},{7,8},{8,9},{9,10},{10,1... | collective-permute-start | bytes 98312 | tf_op jit(solution)/shard_map/ppermute | solution.py:20
  145.7 6.0 %collective-permute-start.6 = (bf16[8,2048]{1,0:T(8,128)(2,1)S(1)}, bf16[8,2048]{1,0:T(8,128)(2,1)S(1)}, u32[]{:S(2)}, u32[]{:S(2)}) collective-permute-start(bf16[8,2048]{1,0:T(8,128)(2,1)S(1)} %collective-permute-done.5), channel_id=1, source_target_pairs={{0,1},{1,2},{2,3},{3,4},{4,5},{5,6},{6,7},{7,8},{8,9},{9,10},{10,1... | collective-permute-start | bytes 98312 | tf_op jit(solution)/shard_map/ppermute | solution.py:20
  151.7 6.0 %collective-permute-start.7 = (bf16[8,2048]{1,0:T(8,128)(2,1)S(1)}, bf16[8,2048]{1,0:T(8,128)(2,1)S(1)}, u32[]{:S(2)}, u32[]{:S(2)}) collective-permute-start(bf16[8,2048]{1,0:T(8,128)(2,1)S(1)} %collective-permute-done.6), channel_id=1, source_target_pairs={{0,1},{1,2},{2,3},{3,4},{4,5},{5,6},{6,7},{7,8},{8,9},{9,10},{10,1... | collective-permute-start | bytes 98312 | tf_op jit(solution)/shard_map/ppermute | solution.py:20
  157.8 6.0 %collective-permute-start.8 = (bf16[8,2048]{1,0:T(8,128)(2,1)S(1)}, bf16[8,2048]{1,0:T(8,128)(2,1)S(1)}, u32[]{:S(2)}, u32[]{:S(2)}) collective-permute-start(bf16[8,2048]{1,0:T(8,128)(2,1)S(1)} %collective-permute-done.7), channel_id=1, source_target_pairs={{0,1},{1,2},{2,3},{3,4},{4,5},{5,6},{6,7},{7,8},{8,9},{9,10},{10,1... | collective-permute-start | bytes 98312 | tf_op jit(solution)/shard_map/ppermute | solution.py:20
  163.8 6.0 %collective-permute-start.9 = (bf16[8,2048]{1,0:T(8,128)(2,1)S(1)}, bf16[8,2048]{1,0:T(8,128)(2,1)S(1)}, u32[]{:S(2)}, u32[]{:S(2)}) collective-permute-start(bf16[8,2048]{1,0:T(8,128)(2,1)S(1)} %collective-permute-done.8), channel_id=1, source_target_pairs={{0,1},{1,2},{2,3},{3,4},{4,5},{5,6},{6,7},{7,8},{8,9},{9,10},{10,1... | collective-permute-start | bytes 98312 | tf_op jit(solution)/shard_map/ppermute | solution.py:20
  169.9 6.0 %collective-permute-start.10 = (bf16[8,2048]{1,0:T(8,128)(2,1)S(1)}, bf16[8,2048]{1,0:T(8,128)(2,1)S(1)}, u32[]{:S(2)}, u32[]{:S(2)}) collective-permute-start(bf16[8,2048]{1,0:T(8,128)(2,1)S(1)} %collective-permute-done.9), channel_id=1, source_target_pairs={{0,1},{1,2},{2,3},{3,4},{4,5},{5,6},{6,7},{7,8},{8,9},{9,10},{10,1... | collective-permute-start | bytes 98312 | tf_op jit(solution)/shard_map/ppermute | solution.py:20
  175.9 6.0 %collective-permute-start.11 = (bf16[8,2048]{1,0:T(8,128)(2,1)S(1)}, bf16[8,2048]{1,0:T(8,128)(2,1)S(1)}, u32[]{:S(2)}, u32[]{:S(2)}) collective-permute-start(bf16[8,2048]{1,0:T(8,128)(2,1)S(1)} %collective-permute-done.10), channel_id=1, source_target_pairs={{0,1},{1,2},{2,3},{3,4},{4,5},{5,6},{6,7},{7,8},{8,9},{9,10},{10,1... | collective-permute-start | bytes 98312 | tf_op jit(solution)/shard_map/ppermute | solution.py:20
  181.9 6.0 %collective-permute-start.12 = (bf16[8,2048]{1,0:T(8,128)(2,1)S(1)}, bf16[8,2048]{1,0:T(8,128)(2,1)S(1)}, u32[]{:S(2)}, u32[]{:S(2)}) collective-permute-start(bf16[8,2048]{1,0:T(8,128)(2,1)S(1)} %collective-permute-done.11), channel_id=1, source_target_pairs={{0,1},{1,2},{2,3},{3,4},{4,5},{5,6},{6,7},{7,8},{8,9},{9,10},{10,1... | collective-permute-start | bytes 98312 | tf_op jit(solution)/shard_map/ppermute | solution.py:20
  188.0 6.0 %collective-permute-start.13 = (bf16[8,2048]{1,0:T(8,128)(2,1)S(1)}, bf16[8,2048]{1,0:T(8,128)(2,1)S(1)}, u32[]{:S(2)}, u32[]{:S(2)}) collective-permute-start(bf16[8,2048]{1,0:T(8,128)(2,1)S(1)} %collective-permute-done.12), channel_id=1, source_target_pairs={{0,1},{1,2},{2,3},{3,4},{4,5},{5,6},{6,7},{7,8},{8,9},{9,10},{10,1... | collective-permute-start | bytes 98312 | tf_op jit(solution)/shard_map/ppermute | solution.py:20
  194.0 6.0 %collective-permute-start.14 = (bf16[8,2048]{1,0:T(8,128)(2,1)S(1)}, bf16[8,2048]{1,0:T(8,128)(2,1)S(1)}, u32[]{:S(2)}, u32[]{:S(2)}) collective-permute-start(bf16[8,2048]{1,0:T(8,128)(2,1)S(1)} %collective-permute-done.13), channel_id=1, source_target_pairs={{0,1},{1,2},{2,3},{3,4},{4,5},{5,6},{6,7},{7,8},{8,9},{9,10},{10,1... | collective-permute-start | bytes 98312 | tf_op jit(solution)/shard_map/ppermute | solution.py:20
